TPU v7x, 16 devices: a 4x2x1 block of a 4x4x8 slice. The times are simulated.
16 devices in a mesh: dp: 2 (over y, z), tp: 8 (over x, core).
Axes of the slice: x: 4, y: 2, z: 1, core: 2. Of those that a mesh axis runs over, the one named last changes fastest.
The devices are a block of a 4x4x8 slice.
Arguments:
- x: bfloat16 [8192, 2048], P(('dp', 'tp')), parts along dimension 0
- dy: bfloat16 [8192, 2048], P(('dp', 'tp')), parts along dimension 0
- pre: bfloat16 [8192, 8192], P('dp', 'tp'), parts along dimension 0
- w_in: bfloat16 [2048, 8192], P(None, 'tp')
- w_down: bfloat16 [8192, 2048], P('tp')
Outputs:
- output 1: bfloat16 [8192, 2048], P(('dp', 'tp')), parts along dimension 0
- output 2: bfloat16 [4096, 8192], P('dp', 'tp'), parts along dimension 0
- output 3: bfloat16 [16384, 2048], P(('dp', 'tp')), parts along dimension 0
There are 2 independent parts. A program takes and returns all parts, laid end to end along the dimension named above; an argument that names none is the same for every part.
All inputs are finite; a program needn't handle non-finite values.
Results may differ from a plain program's by a relative error of at most 0.012.
Values are sent between devices in bfloat16 or wider.
A program may use at most 768 MiB of HBM per device.

v0:
```python
import functools

import jax
import jax.numpy as jnp
from jax import lax
from jax.experimental import pallas as pl
from jax.experimental.pallas import tpu as pltpu
from jax.sharding import PartitionSpec as P

MESH = pl.DeviceIdType.MESH
F32, BF16 = jnp.float32, jnp.bfloat16
CORES = 2
PAIRS = 8
PIECES = 4
NT = (((1,), (1,)), ((), ()))
TN = (((0,), (0,)), ((), ()))
DY, X = 0, 1
VMEM_LIMIT = 53 * 2**20


def gelu_and_slope(p):
    c = 0.7978845608028654
    sq = p * p
    t = jnp.tanh(c * (p + 0.044715 * (sq * p)))
    cdf = 0.5 * (1.0 + t)
    slope = cdf + (0.5 * p) * (1.0 - t * t) * (c * (1.0 + 0.134145 * sq))
    return p * cdf, slope


def kernel(
    n, x, dy, pre, w_in, w_down,
    dx, dw_in, dw_down, x_all, dy_all, rs_pair, rs_ring,
    acc_in, acc_down, dpre, stash, st_ring, rows_buf, pre_buf, hid, tmp, chain_buf,
    ring_s, ring_r, pair_s, pair_r, rsp_s, rsp_r, rsg_s, rsg_r, ch_s, ch_r, w_sem, pre_sem, ld_sem,
):
    wi, wd, st_pair = dw_in, dw_down, dx
    me = lax.axis_index("tp")
    core = lax.rem(me, CORES)
    chip = me // CORES
    chips = n // CORES
    right = lax.rem(me + CORES, n)
    left = lax.rem(me + n - CORES, n)
    partner = me + 1 - 2 * core
    size, ff = x.shape[0], pre.shape[1]
    d = x.shape[1]
    half = size // 2
    piece = half // PIECES

    def place(i):
        q, r = i // 2, i % 2
        odd = ((q + 1) // 2) % 2
        off = odd * (chips - 1 + 2 * r) + 2 * (q // 3)
        turned = (q // 2) * (1 - q // 3)
        return lax.rem(chip + off, chips), r + turned * (1 - 2 * r)

    def at(ref, shard, h):
        return ref.at[shard, pl.ds(pl.multiple_of(h * half, half), half)]

    def of_core(ref, i, k):
        c, h = place(i)
        return at(ref, c * CORES + k, h)

    own = (dy, x)
    gathered = (dy_all, x_all)

    def own_half(w, h):
        return own[w].at[pl.ds(h * half, half)]

    def remote(src, dst, s, r, dev):
        return pltpu.make_async_remote_copy(
            src_ref=src, dst_ref=dst, send_sem=s, recv_sem=r, device_id={"tp": dev}, device_id_type=MESH
        )

    def ring_own(w, j):
        h = {2: 0, 3: 1, 4: 1, 5: 0}[j]
        return remote(own_half(w, h), at(gathered[w], me, h), ring_s.at[w, j], ring_r.at[w, j], right if j % 2 == 0 else left)

    def ring_relay(w, j):
        ref = of_core(gathered[w], j - 4, core)
        return remote(ref, ref, ring_s.at[w, j], ring_r.at[w, j], right if j % 2 == 0 else left)

    def ring_send(w, j):
        return ring_own(w, j) if j < 6 else ring_relay(w, j)

    def ring_got(w, j):
        ref = of_core(gathered[w], j, core)
        return remote(ref, ref, ring_s.at[w, j], ring_r.at[w, j], right)

    def to_partner(w, j):
        src = own_half(w, j) if j < 2 else of_core(gathered[w], j, core)
        return remote(src, of_core(gathered[w], j, core), pair_s.at[w, j], pair_r.at[w, j], partner)

    def from_partner(w, j):
        ref = of_core(gathered[w], j, 1 - core)
        return remote(ref, ref, pair_s.at[w, j], pair_r.at[w, j], partner)

    def service(w, j):
        ring_got(w, j).wait_recv()
        if j < 4:
            ring_relay(w, j + 4).start()
        to_partner(w, j).start()

    def load(src, dst, sem):
        c = pltpu.make_async_copy(src, dst, sem)
        c.start()
        return c

    def load_rows(w, j):
        from_partner(w, j).wait_recv()
        load(of_core(gathered[w], j, 1 - core), rows_buf.at[pl.ds(0, half)], ld_sem.at[0])
        c, h = place(j)

        @pl.when(j < 2)
        def _():
            load(own[w].at[pl.ds(pl.multiple_of(h * half, half), half)], rows_buf.at[pl.ds(half, half)], ld_sem.at[1])

        @pl.when(j >= 2)
        def _():
            load(of_core(gathered[w], j, core), rows_buf.at[pl.ds(half, half)], ld_sem.at[1])

        for b in range(2):
            pltpu.make_async_copy(rows_buf.at[pl.ds(0, half)], rows_buf.at[pl.ds(b * half, half)], ld_sem.at[b]).wait()

    def pre_load(j, b):
        c, h = place(j)
        where = (1 - core) if b == 0 else core
        start = pl.multiple_of((c * CORES + where) * size + h * half, half)
        return pltpu.make_async_copy(
            pre.at[pl.ds(start, half)], pre_buf.at[j % 2, pl.ds(b * half, half)], pre_sem.at[j % 2, b]
        )

    def pair_sum(j):
        return remote(st_pair.at[pl.ds(pl.multiple_of(j % 2 * half, half), half)], rs_pair.at[j], rsp_s.at[j], rsp_r.at[j], partner)

    def ring_sum(j):
        dev = lax.rem(me + n - CORES + 2 * CORES * (j % 2), n)
        return remote(st_ring.at[j - 4], rs_ring.at[j - 4], rsg_s.at[j - 4], rsg_r.at[j - 4], dev)

    def chain_send(b, q):
        ref = (b, pl.ds(q * piece, piece))
        return remote(st_ring.at[ref], chain_buf.at[ref], ch_s.at[b, q], ch_r.at[b, q], left if b == 0 else right)

    barrier = pltpu.get_barrier_semaphore()
    for dev in (left, right, partner):
        pl.semaphore_signal(barrier, inc=1, device_id={"tp": dev}, device_id_type=MESH)
    pl.semaphore_wait(barrier, 3)

    for j in (2, 3, 4, 5):
        ring_own(DY, j).start()
    for j in (0, 1):
        to_partner(DY, j).start()
    for b in range(2):
        pre_load(0, b).start()
    load(w_down, wd, w_sem.at[0])
    load(w_in, wi, w_sem.at[1])

    @pl.loop(0, ff, step=64)
    def _(r):
        acc_down[pl.ds(pl.multiple_of(r, 64), 64)] = jnp.zeros((64, d), F32)

    @pl.loop(0, d, step=128)
    def _(r):
        acc_in[pl.ds(pl.multiple_of(r, 128), 128)] = jnp.zeros((128, ff), F32)

    pltpu.make_async_copy(w_down, wd, w_sem.at[0]).wait()
    pltpu.make_async_copy(w_in, wi, w_sem.at[1]).wait()

    tile = 256

    @pl.loop(0, PAIRS)
    def _(i):
        slot = i % 2

        @pl.when(i == 2)
        def _():
            service(DY, 2)
            service(DY, 3)
            ring_own(X, 2).start()
            ring_own(X, 3).start()
            to_partner(X, 0).start()
            to_partner(X, 1).start()

        @pl.when(i == 4)
        def _():
            service(DY, 4)
            service(DY, 5)

        @pl.when(i == 6)
        def _():
            service(DY, 6)
            service(DY, 7)
            ring_own(X, 4).start()
            ring_own(X, 5).start()

        @pl.when(i < PAIRS - 1)
        def _():
            for b in range(2):
                pre_load(i + 1, b).start()

        load_rows(DY, i)
        for b in range(2):
            pre_load(i, b).wait()

        @pl.loop(0, ff, step=tile)
        def _(f):
            fs = pl.ds(pl.multiple_of(f, tile), tile)
            dh = lax.dot_general(rows_buf[...], wd[fs, :], NT, preferred_element_type=F32)
            h, slope = gelu_and_slope(pre_buf[slot, :, fs].astype(F32))
            dpre[i, :, fs] = (dh * slope).astype(BF16)
            hid[:, fs] = h.astype(BF16)

        @pl.when(i >= 2)
        def _():
            pair_sum(i - 2).wait_send()

        @pl.loop(0, d, step=2 * tile)
        def _(c):
            cs = pl.ds(pl.multiple_of(c, 2 * tile), 2 * tile)
            o = lax.dot_general(dpre[i, 0:half, :], wi[cs, :], NT, preferred_element_type=F32)
            st_pair[pl.ds(pl.multiple_of(slot * half, half), half), cs] = o.astype(BF16)

        pair_sum(i).start()

        @pl.loop(0, ff, step=tile)
        def _(f):
            fs = pl.ds(pl.multiple_of(f, tile), tile)

            for c in range(0, d, 2 * tile):
                acc_down[fs, c : c + 2 * tile] += lax.dot_general(
                    hid[:, fs], rows_buf[:, c : c + 2 * tile], TN, preferred_element_type=F32
                )

        pair_sum(i).wait_recv()
        load(rs_pair.at[i], tmp, ld_sem.at[0]).wait()

        def mine(c):
            cs = pl.ds(pl.multiple_of(c, 2 * tile), 2 * tile)
            o = lax.dot_general(dpre[i, half : 2 * half, :], wi[cs, :], NT, preferred_element_type=F32)
            return cs, o + tmp[:, cs].astype(F32)

        @pl.when(i < 4)
        def _():
            @pl.loop(0, d, step=2 * tile)
            def _(c):
                cs, o = mine(c)
                stash[i, :, cs] = o

        @pl.when(i >= 4)
        def _():
            @pl.loop(0, d, step=2 * tile)
            def _(c):
                cs, o = mine(c)
                st_ring[i - 4, :, cs] = o.astype(BF16)

            ring_sum(i).start()

    service(X, 2)
    service(X, 3)

    for b in range(2):
        pair_sum(PAIRS - 2 + b).wait_send()

    @pl.loop(0, ff, step=32)
    def _(r):
        rs = pl.ds(pl.multiple_of(r, 32), 32)
        dw_down[rs] = acc_down[rs].astype(BF16)

    def chain(b):
        ring_sum(6 + b).wait_recv()
        load(rs_ring.at[2 + b], tmp, ld_sem.at[0]).wait()
        ring_sum(4 + b).wait_send()

        @pl.loop(0, half, step=32)
        def _(r):
            rs = pl.ds(pl.multiple_of(r, 32), 32)
            st_ring[b, rs] = (stash[2 + b, rs] + tmp[rs].astype(F32)).astype(BF16)

        for q in range(PIECES):
            chain_send(b, q).start()

    def direct(b):
        ring_sum(4 + b).wait_recv()
        load(rs_ring.at[b], tmp, ld_sem.at[0]).wait()

        @pl.loop(0, half, step=32)
        def _(r):
            rs = pl.ds(pl.multiple_of(r, 32), 32)
            stash[1 - b, rs] += tmp[rs].astype(F32)

    @pl.loop(0, PAIRS)
    def _(i):
        @pl.when(i == 4)
        def _():
            direct(0)
            direct(1)
            chain(0)
            chain(1)
            service(X, 4)
            service(X, 5)

        @pl.when(i == 6)
        def _():
            service(X, 6)
            service(X, 7)

        load_rows(X, i)

        @pl.loop(0, d, step=tile)
        def _(c):
            cs = pl.ds(pl.multiple_of(c, tile), tile)

            for f in range(0, ff, 2 * tile):
                acc_in[cs, f : f + 2 * tile] += lax.dot_general(
                    rows_buf[:, cs], dpre[i, :, f : f + 2 * tile], TN, preferred_element_type=F32
                )

    @pl.loop(0, d, step=64)
    def _(r):
        rs = pl.ds(pl.multiple_of(r, 64), 64)
        dw_in[rs] = acc_in[rs].astype(BF16)

    for q in range(PIECES):
        for b in range(2):
            chain_send(b, q).wait_recv()
            rs = pl.ds(q * piece, piece)
            dx[pl.ds(b * half + q * piece, piece)] = (stash[b, rs] + chain_buf[b, rs].astype(F32)).astype(BF16)

    for w in (DY, X):
        for j in range(2, PAIRS):
            ring_send(w, j).wait_send()
        for j in range(PAIRS):
            to_partner(w, j).wait_send()
    for j in (6, 7):
        ring_sum(j).wait_send()
    for b in range(2):
        for q in range(PIECES):
            chain_send(b, q).wait_send()


def results(*refs):
    count = len(refs) // 2
    ins, outs, sem = refs[:count], refs[count : 2 * count], refs[-1]
    copies = [pltpu.make_async_copy(a, b, sem.at[i]) for i, (a, b) in enumerate(zip(ins, outs))]
    for c in copies:
        c.start()
    for c in copies:
        c.wait()


def solution(mesh):
    n = mesh.shape["tp"]

    def step(x, dy, pre, w_in, w_down):
        (size, d), ff = x.shape, pre.shape[1]
        half = size // 2
        any_space = pl.BlockSpec(memory_space=pl.ANY)
        shapes = ((size, d), (d, ff), (ff, d))
        dma = pltpu.SemaphoreType.DMA
        outs = pl.pallas_call(
            functools.partial(kernel, n),
            out_shape=[pltpu.VMEM(s, BF16) for s in shapes]
            + [
                jax.ShapeDtypeStruct(s, BF16)
                for s in ((n, size, d), (n, size, d), (PAIRS, half, d), (4, half, d))
            ],
            in_specs=[any_space] * 5,
            out_specs=[pl.BlockSpec(memory_space=pltpu.VMEM)] * 3 + [any_space] * 4,
            scratch_shapes=[
                pltpu.VMEM((d, ff), F32),
                pltpu.VMEM((ff, d), F32),
                pltpu.VMEM((PAIRS, size, ff), BF16),
                pltpu.VMEM((4, half, d), F32),
                pltpu.VMEM((4, half, d), BF16),
                pltpu.VMEM((size, d), BF16),
                pltpu.VMEM((2, size, ff), BF16),
                pltpu.VMEM((size, ff), BF16),
                pltpu.VMEM((half, d), BF16),
                pltpu.VMEM((2, half, d), BF16),
                dma((2, PAIRS)), dma((2, PAIRS)), dma((2, PAIRS)), dma((2, PAIRS)),
                dma((PAIRS,)), dma((PAIRS,)), dma((4,)), dma((4,)), dma((2, PIECES)), dma((2, PIECES)),
                dma((2,)), dma((2, 2)), dma((2,)),
            ],
            compiler_params=pltpu.CompilerParams(collective_id=0, has_side_effects=True, vmem_limit_bytes=VMEM_LIMIT),
            name="mlp_backward",
        )(x, dy, pre, w_in, w_down)
        return tuple(
            pl.pallas_call(
                results,
                out_shape=[jax.ShapeDtypeStruct(s, BF16) for s in shapes],
                in_specs=[pl.BlockSpec(memory_space=pltpu.VMEM)] * 3,
                out_specs=[any_space] * 3,
                scratch_shapes=[dma((3,))],
                compiler_params=pltpu.CompilerParams(vmem_limit_bytes=2**20),
                name="results",
            )(*(pltpu.with_memory_space_constraint(o, pltpu.VMEM) for o in outs[:3]))
        )

    rows = P(("dp", "tp"), None)
    return jax.shard_map(
        step,
        mesh=mesh,
        in_specs=(rows, rows, P("dp", "tp"), P(None, "tp"), P("tp", None)),
        out_specs=(rows, P("dp", "tp"), rows),
        check_vma=False,
    )
```

profile of v0, /device:TPU:112, one launch (start us, length us, event | category | flops | bytes accessed | tf_op | source)
XLA Modules:
  0.0 213.5 jit_solution(9369559950634534711)
XLA Ops:
  0.6 208.8 %mlp_backward.1 = (bf16[512,2048]{1,0:T(8,128)(2,1)S(1)}, bf16[2048,1024]{1,0:T(8,128)(2,1)S(1)}, bf16[1024,2048]{1,0:T(8,128)(2,1)S(1)}, bf16[8,512,2048]{2,1,0...) custom-call(bf16[512,2048]{1,0:T(8,128)(2,1)} %x.1, ...), custom_call_target="tpu_custom_call" | custom-call | tf_op jit(solution)/shard_map/mlp_backward/pallas_call | solution.py:359
  209.4 4.1 %results.1 = (bf16[512,2048]{1,0:T(8,128)(2,1)}, bf16[2048,1024]{1,0:T(8,128)(2,1)}, bf16[1024,2048]{1,0:T(8,128)(2,1)}) custom-call(bf16[512,2048]{1,0:T(8,128)(2,1)S(1)} %get-tuple-element.6.refs_0_, bf16[2048,1024]{1,0:T(8,128)(2,1)S(1)} %get-tuple-element.7.refs_1_, bf16[1024,2048]{1,0:T(8,128)(2,1)S(1)} %get-tuple-element.8.refs_2_), custom_call_target="tpu_custom_call" | custom-call | tf_op jit(solution)/shard_map/results/pallas_call | solution.py:387
where the time goes:
time: 215 us; the launch traced here: 214 us
  Pallas kernels  213 us (99%)
    pallas_call x1, Pallas kernels, step(): pl.pallas_call(functools.partial(kernel, n), out_shape=[pltpu.VMEM(s, BF1...  209 us

commit v1 on v0

--- a/solution.py
+++ b/solution.py
@@ -11,7 +11,7 @@
 F32, BF16 = jnp.float32, jnp.bfloat16
 CORES = 2
 PAIRS = 8
-PIECES = 4
+PIECES = 2
 NT = (((1,), (1,)), ((), ()))
 TN = (((0,), (0,)), ((), ()))
 DY, X = 0, 1
@@ -184,13 +184,13 @@
         def _():
             service(DY, 4)
             service(DY, 5)
+            ring_own(X, 4).start()
+            ring_own(X, 5).start()
 
         @pl.when(i == 6)
         def _():
             service(DY, 6)
             service(DY, 7)
-            ring_own(X, 4).start()
-            ring_own(X, 5).start()
 
         @pl.when(i < PAIRS - 1)
         def _():
@@ -319,12 +319,6 @@
         rs = pl.ds(pl.multiple_of(r, 64), 64)
         dw_in[rs] = acc_in[rs].astype(BF16)
 
-    for q in range(PIECES):
-        for b in range(2):
-            chain_send(b, q).wait_recv()
-            rs = pl.ds(q * piece, piece)
-            dx[pl.ds(b * half + q * piece, piece)] = (stash[b, rs] + chain_buf[b, rs].astype(F32)).astype(BF16)
-
     for w in (DY, X):
         for j in range(2, PAIRS):
             ring_send(w, j).wait_send()
@@ -332,6 +326,13 @@
             to_partner(w, j).wait_send()
     for j in (6, 7):
         ring_sum(j).wait_send()
+
+    for q in range(PIECES):
+        for b in range(2):
+            chain_send(b, q).wait_recv()
+            rs = pl.ds(q * piece, piece)
+            dx[pl.ds(b * half + q * piece, piece)] = (stash[b, rs] + chain_buf[b, rs].astype(F32)).astype(BF16)
+
     for b in range(2):
         for q in range(PIECES):
             chain_send(b, q).wait_send()
@@ -340,7 +341,12 @@
 def results(*refs):
     count = len(refs) // 2
     ins, outs, sem = refs[:count], refs[count : 2 * count], refs[-1]
-    copies = [pltpu.make_async_copy(a, b, sem.at[i]) for i, (a, b) in enumerate(zip(ins, outs))]
+    copies = []
+    for a, b in zip(ins, outs):
+        rows = a.shape[0] // 2
+        for i in range(2):
+            rs = pl.ds(i * rows, rows)
+            copies.append(pltpu.make_async_copy(a.at[rs], b.at[rs], sem.at[len(copies)]))
     for c in copies:
         c.start()
     for c in copies:
@@ -389,7 +395,7 @@
                 out_shape=[jax.ShapeDtypeStruct(s, BF16) for s in shapes],
                 in_specs=[pl.BlockSpec(memory_space=pltpu.VMEM)] * 3,
                 out_specs=[any_space] * 3,
-                scratch_shapes=[dma((3,))],
+                scratch_shapes=[dma((6,))],
                 compiler_params=pltpu.CompilerParams(vmem_limit_bytes=2**20),
                 name="results",
             )(*(pltpu.with_memory_space_constraint(o, pltpu.VMEM) for o in outs[:3]))

time: 215 us -> 214 us (level)
  no operation moved by 1% of the time
where the time goes in v1:
time: 214 us; the launch traced here: 213 us
  Pallas kernels  213 us (100%)
    pallas_call x1, Pallas kernels, step(): pl.pallas_call(functools.partial(kernel, n), out_shape=[pltpu.VMEM(s, BF1...  209 us

profile of v1, /device:TPU:112, one launch (start us, length us, event | category | flops | bytes accessed | tf_op | source)
XLA Modules:
  0.0 213.2 jit_solution(6585486035853549904)
XLA Ops:
  0.6 208.6 %mlp_backward.1 = (bf16[512,2048]{1,0:T(8,128)(2,1)S(1)}, bf16[2048,1024]{1,0:T(8,128)(2,1)S(1)}, bf16[1024,2048]{1,0:T(8,128)(2,1)S(1)}, bf16[8,512,2048]{2,1,0...) custom-call(bf16[512,2048]{1,0:T(8,128)(2,1)} %x.1, ...), custom_call_target="tpu_custom_call" | custom-call | tf_op jit(solution)/shard_map/mlp_backward/pallas_call | solution.py:365
  209.2 4.0 %results.1 = (bf16[512,2048]{1,0:T(8,128)(2,1)}, bf16[2048,1024]{1,0:T(8,128)(2,1)}, bf16[1024,2048]{1,0:T(8,128)(2,1)}) custom-call(bf16[512,2048]{1,0:T(8,128)(2,1)S(1)} %get-tuple-element.6.refs_0_, bf16[2048,1024]{1,0:T(8,128)(2,1)S(1)} %get-tuple-element.7.refs_1_, bf16[1024,2048]{1,0:T(8,128)(2,1)S(1)} %get-tuple-element.8.refs_2_), custom_call_target="tpu_custom_call" | custom-call | tf_op jit(solution)/shard_map/results/pallas_call | solution.py:393

commit v2 on v1

--- a/solution.py
+++ b/solution.py
@@ -29,8 +29,8 @@
 
 def kernel(
     n, x, dy, pre, w_in, w_down,
-    dx, dw_in, dw_down, x_all, dy_all, rs_pair, rs_ring,
-    acc_in, acc_down, dpre, stash, st_ring, rows_buf, pre_buf, hid, tmp, chain_buf,
+    dx, dw_in, dw_down, x_all, dy_all,
+    acc_in, acc_down, dpre, stash, st_ring, rows_buf, pre_buf, hid, pair_buf, ring_buf, chain_buf,
     ring_s, ring_r, pair_s, pair_r, rsp_s, rsp_r, rsg_s, rsg_r, ch_s, ch_r, w_sem, pre_sem, ld_sem,
 ):
     wi, wd, st_pair = dw_in, dw_down, dx
@@ -105,21 +105,32 @@
         c.start()
         return c
 
-    def load_rows(w, j):
+    def start_rows(w, j):
         from_partner(w, j).wait_recv()
-        load(of_core(gathered[w], j, 1 - core), rows_buf.at[pl.ds(0, half)], ld_sem.at[0])
+        slot = j % 2
+        load(of_core(gathered[w], j, 1 - core), rows_buf.at[slot, pl.ds(0, half)], ld_sem.at[slot, 0])
         c, h = place(j)
 
         @pl.when(j < 2)
         def _():
-            load(own[w].at[pl.ds(pl.multiple_of(h * half, half), half)], rows_buf.at[pl.ds(half, half)], ld_sem.at[1])
+            src = own[w].at[pl.ds(pl.multiple_of(h * half, half), half)]
+            load(src, rows_buf.at[slot, pl.ds(half, half)], ld_sem.at[slot, 1])
 
         @pl.when(j >= 2)
         def _():
-            load(of_core(gathered[w], j, core), rows_buf.at[pl.ds(half, half)], ld_sem.at[1])
-
+            load(of_core(gathered[w], j, core), rows_buf.at[slot, pl.ds(half, half)], ld_sem.at[slot, 1])
+
+    def rows_of(w, j):
+        @pl.when(j % 2 == 0)
+        def _():
+            start_rows(w, j)
+            start_rows(w, j + 1)
+
+        slot = j % 2
         for b in range(2):
-            pltpu.make_async_copy(rows_buf.at[pl.ds(0, half)], rows_buf.at[pl.ds(b * half, half)], ld_sem.at[b]).wait()
+            ref = rows_buf.at[slot, pl.ds(b * half, half)]
+            pltpu.make_async_copy(ref, ref, ld_sem.at[slot, b]).wait()
+        return rows_buf.at[slot]
 
     def pre_load(j, b):
         c, h = place(j)
@@ -130,11 +141,11 @@
         )
 
     def pair_sum(j):
-        return remote(st_pair.at[pl.ds(pl.multiple_of(j % 2 * half, half), half)], rs_pair.at[j], rsp_s.at[j], rsp_r.at[j], partner)
+        return remote(st_pair.at[pl.ds(pl.multiple_of(j % 2 * half, half), half)], pair_buf.at[j % 2], rsp_s.at[j], rsp_r.at[j], partner)
 
     def ring_sum(j):
         dev = lax.rem(me + n - CORES + 2 * CORES * (j % 2), n)
-        return remote(st_ring.at[j - 4], rs_ring.at[j - 4], rsg_s.at[j - 4], rsg_r.at[j - 4], dev)
+        return remote(st_ring.at[j - 4], ring_buf.at[j - 4], rsg_s.at[j - 4], rsg_r.at[j - 4], dev)
 
     def chain_send(b, q):
         ref = (b, pl.ds(q * piece, piece))
@@ -197,14 +208,14 @@
             for b in range(2):
                 pre_load(i + 1, b).start()
 
-        load_rows(DY, i)
+        rows = rows_of(DY, i)
         for b in range(2):
             pre_load(i, b).wait()
 
         @pl.loop(0, ff, step=tile)
         def _(f):
             fs = pl.ds(pl.multiple_of(f, tile), tile)
-            dh = lax.dot_general(rows_buf[...], wd[fs, :], NT, preferred_element_type=F32)
+            dh = lax.dot_general(rows[...], wd[fs, :], NT, preferred_element_type=F32)
             h, slope = gelu_and_slope(pre_buf[slot, :, fs].astype(F32))
             dpre[i, :, fs] = (dh * slope).astype(BF16)
             hid[:, fs] = h.astype(BF16)
@@ -227,16 +238,15 @@
 
             for c in range(0, d, 2 * tile):
                 acc_down[fs, c : c + 2 * tile] += lax.dot_general(
-                    hid[:, fs], rows_buf[:, c : c + 2 * tile], TN, preferred_element_type=F32
+                    hid[:, fs], rows[:, c : c + 2 * tile], TN, preferred_element_type=F32
                 )
 
         pair_sum(i).wait_recv()
-        load(rs_pair.at[i], tmp, ld_sem.at[0]).wait()
 
         def mine(c):
             cs = pl.ds(pl.multiple_of(c, 2 * tile), 2 * tile)
             o = lax.dot_general(dpre[i, half : 2 * half, :], wi[cs, :], NT, preferred_element_type=F32)
-            return cs, o + tmp[:, cs].astype(F32)
+            return cs, o + pair_buf[slot, :, cs].astype(F32)
 
         @pl.when(i < 4)
         def _():
@@ -267,25 +277,23 @@
 
     def chain(b):
         ring_sum(6 + b).wait_recv()
-        load(rs_ring.at[2 + b], tmp, ld_sem.at[0]).wait()
         ring_sum(4 + b).wait_send()
 
         @pl.loop(0, half, step=32)
         def _(r):
             rs = pl.ds(pl.multiple_of(r, 32), 32)
-            st_ring[b, rs] = (stash[2 + b, rs] + tmp[rs].astype(F32)).astype(BF16)
+            st_ring[b, rs] = (stash[2 + b, rs] + ring_buf[2 + b, rs].astype(F32)).astype(BF16)
 
         for q in range(PIECES):
             chain_send(b, q).start()
 
     def direct(b):
         ring_sum(4 + b).wait_recv()
-        load(rs_ring.at[b], tmp, ld_sem.at[0]).wait()
 
         @pl.loop(0, half, step=32)
         def _(r):
             rs = pl.ds(pl.multiple_of(r, 32), 32)
-            stash[1 - b, rs] += tmp[rs].astype(F32)
+            stash[1 - b, rs] += ring_buf[b, rs].astype(F32)
 
     @pl.loop(0, PAIRS)
     def _(i):
@@ -303,7 +311,7 @@
             service(X, 6)
             service(X, 7)
 
-        load_rows(X, i)
+        rows = rows_of(X, i)
 
         @pl.loop(0, d, step=tile)
         def _(c):
@@ -311,7 +319,7 @@
 
             for f in range(0, ff, 2 * tile):
                 acc_in[cs, f : f + 2 * tile] += lax.dot_general(
-                    rows_buf[:, cs], dpre[i, :, f : f + 2 * tile], TN, preferred_element_type=F32
+                    rows[:, cs], dpre[i, :, f : f + 2 * tile], TN, preferred_element_type=F32
                 )
 
     @pl.loop(0, d, step=64)
@@ -367,24 +375,25 @@
             out_shape=[pltpu.VMEM(s, BF16) for s in shapes]
             + [
                 jax.ShapeDtypeStruct(s, BF16)
-                for s in ((n, size, d), (n, size, d), (PAIRS, half, d), (4, half, d))
+                for s in ((n, size, d), (n, size, d))
             ],
             in_specs=[any_space] * 5,
-            out_specs=[pl.BlockSpec(memory_space=pltpu.VMEM)] * 3 + [any_space] * 4,
+            out_specs=[pl.BlockSpec(memory_space=pltpu.VMEM)] * 3 + [any_space] * 2,
             scratch_shapes=[
                 pltpu.VMEM((d, ff), F32),
                 pltpu.VMEM((ff, d), F32),
                 pltpu.VMEM((PAIRS, size, ff), BF16),
                 pltpu.VMEM((4, half, d), F32),
                 pltpu.VMEM((4, half, d), BF16),
-                pltpu.VMEM((size, d), BF16),
+                pltpu.VMEM((2, size, d), BF16),
                 pltpu.VMEM((2, size, ff), BF16),
                 pltpu.VMEM((size, ff), BF16),
-                pltpu.VMEM((half, d), BF16),
+                pltpu.VMEM((2, half, d), BF16),
+                pltpu.VMEM((4, half, d), BF16),
                 pltpu.VMEM((2, half, d), BF16),
                 dma((2, PAIRS)), dma((2, PAIRS)), dma((2, PAIRS)), dma((2, PAIRS)),
                 dma((PAIRS,)), dma((PAIRS,)), dma((4,)), dma((4,)), dma((2, PIECES)), dma((2, PIECES)),
-                dma((2,)), dma((2, 2)), dma((2,)),
+                dma((2,)), dma((2, 2)), dma((2, 2)),
             ],
             compiler_params=pltpu.CompilerParams(collective_id=0, has_side_effects=True, vmem_limit_bytes=VMEM_LIMIT),
             name="mlp_backward",

time: 214 us -> 213 us (level)
  no operation moved by 1% of the time
where the time goes in v2:
time: 213 us
  Pallas kernels  213 us (100%)
    pallas_call x1, Pallas kernels, step(): pl.pallas_call(functools.partial(kernel, n), out_shape=[pltpu.VMEM(s, BF1...  209 us

profile of v2, /device:TPU:112, one launch (start us, length us, event | category | flops | bytes accessed | tf_op | source)
XLA Modules:
  0.0 213.3 jit_solution(7316015792201926785)
XLA Ops:
  0.6 208.6 %mlp_backward.1 = (bf16[512,2048]{1,0:T(8,128)(2,1)S(1)}, bf16[2048,1024]{1,0:T(8,128)(2,1)S(1)}, bf16[1024,2048]{1,0:T(8,128)(2,1)S(1)}, bf16[8,512,2048]{2,1,0:T(8,128)(2,1)}, bf16[8,512,2048]{2,1,0:T(8,128)(2,1)}) custom-call(bf16[512,2048]{1,0:T(8,128)(2,1)} %x.1, bf16[512,2048]{1,0:T(8,128)(2,1)} %dy.1, bf16[4096,1024]{1,0:T(8,128)(2,1)} %pre.1, ...), custom_call_target="tpu_custom_call" | custom-call | tf_op jit(solution)/shard_map/mlp_backward/pallas_call | solution.py:373
  209.2 4.0 %results.1 = (bf16[512,2048]{1,0:T(8,128)(2,1)}, bf16[2048,1024]{1,0:T(8,128)(2,1)}, bf16[1024,2048]{1,0:T(8,128)(2,1)}) custom-call(bf16[512,2048]{1,0:T(8,128)(2,1)S(1)} %get-tuple-element.6.refs_0_, bf16[2048,1024]{1,0:T(8,128)(2,1)S(1)} %get-tuple-element.7.refs_1_, bf16[1024,2048]{1,0:T(8,128)(2,1)S(1)} %get-tuple-element.8.refs_2_), custom_call_target="tpu_custom_call" | custom-call | tf_op jit(solution)/shard_map/results/pallas_call | solution.py:402

commit v3 on v2

--- a/solution.py
+++ b/solution.py
@@ -11,7 +11,7 @@
 F32, BF16 = jnp.float32, jnp.bfloat16
 CORES = 2
 PAIRS = 8
-PIECES = 2
+LAST = 32
 NT = (((1,), (1,)), ((), ()))
 TN = (((0,), (0,)), ((), ()))
 DY, X = 0, 1
@@ -31,7 +31,7 @@
     n, x, dy, pre, w_in, w_down,
     dx, dw_in, dw_down, x_all, dy_all,
     acc_in, acc_down, dpre, stash, st_ring, rows_buf, pre_buf, hid, pair_buf, ring_buf, chain_buf,
-    ring_s, ring_r, pair_s, pair_r, rsp_s, rsp_r, rsg_s, rsg_r, ch_s, ch_r, w_sem, pre_sem, ld_sem,
+    ring_s, ring_r, pair_s, pair_r, rsp_s, rsp_r, sum_s, rsg_r, ch_r, w_sem, pre_sem, ld_sem,
 ):
     wi, wd, st_pair = dw_in, dw_down, dx
     me = lax.axis_index("tp")
@@ -44,7 +44,6 @@
     size, ff = x.shape[0], pre.shape[1]
     d = x.shape[1]
     half = size // 2
-    piece = half // PIECES
 
     def place(i):
         q, r = i // 2, i % 2
@@ -73,26 +72,26 @@
 
     def ring_own(w, j):
         h = {2: 0, 3: 1, 4: 1, 5: 0}[j]
-        return remote(own_half(w, h), at(gathered[w], me, h), ring_s.at[w, j], ring_r.at[w, j], right if j % 2 == 0 else left)
+        return remote(own_half(w, h), at(gathered[w], me, h), ring_s.at[0], ring_r.at[w, j - 2], right if j % 2 == 0 else left)
 
     def ring_relay(w, j):
         ref = of_core(gathered[w], j - 4, core)
-        return remote(ref, ref, ring_s.at[w, j], ring_r.at[w, j], right if j % 2 == 0 else left)
+        return remote(ref, ref, ring_s.at[0], ring_r.at[w, j - 2], right if j % 2 == 0 else left)
 
     def ring_send(w, j):
         return ring_own(w, j) if j < 6 else ring_relay(w, j)
 
     def ring_got(w, j):
         ref = of_core(gathered[w], j, core)
-        return remote(ref, ref, ring_s.at[w, j], ring_r.at[w, j], right)
+        return remote(ref, ref, ring_s.at[0], ring_r.at[w, j - 2], right)
 
     def to_partner(w, j):
         src = own_half(w, j) if j < 2 else of_core(gathered[w], j, core)
-        return remote(src, of_core(gathered[w], j, core), pair_s.at[w, j], pair_r.at[w, j], partner)
+        return remote(src, of_core(gathered[w], j, core), pair_s.at[0], pair_r.at[j], partner)
 
     def from_partner(w, j):
         ref = of_core(gathered[w], j, 1 - core)
-        return remote(ref, ref, pair_s.at[w, j], pair_r.at[w, j], partner)
+        return remote(ref, ref, pair_s.at[0], pair_r.at[j], partner)
 
     def service(w, j):
         ring_got(w, j).wait_recv()
@@ -108,28 +107,21 @@
     def start_rows(w, j):
         from_partner(w, j).wait_recv()
         slot = j % 2
-        load(of_core(gathered[w], j, 1 - core), rows_buf.at[slot, pl.ds(0, half)], ld_sem.at[slot, 0])
+        load(of_core(gathered[w], j, 1 - core), rows_buf.at[slot, pl.ds(0, half)], ld_sem.at[slot])
         c, h = place(j)
 
         @pl.when(j < 2)
         def _():
             src = own[w].at[pl.ds(pl.multiple_of(h * half, half), half)]
-            load(src, rows_buf.at[slot, pl.ds(half, half)], ld_sem.at[slot, 1])
+            load(src, rows_buf.at[slot, pl.ds(half, half)], ld_sem.at[slot])
 
         @pl.when(j >= 2)
         def _():
-            load(of_core(gathered[w], j, core), rows_buf.at[slot, pl.ds(half, half)], ld_sem.at[slot, 1])
-
-    def rows_of(w, j):
-        @pl.when(j % 2 == 0)
-        def _():
-            start_rows(w, j)
-            start_rows(w, j + 1)
-
+            load(of_core(gathered[w], j, core), rows_buf.at[slot, pl.ds(half, half)], ld_sem.at[slot])
+
+    def rows_of(j):
         slot = j % 2
-        for b in range(2):
-            ref = rows_buf.at[slot, pl.ds(b * half, half)]
-            pltpu.make_async_copy(ref, ref, ld_sem.at[slot, b]).wait()
+        pltpu.make_async_copy(rows_buf.at[slot], rows_buf.at[slot], ld_sem.at[slot]).wait()
         return rows_buf.at[slot]
 
     def pre_load(j, b):
@@ -137,19 +129,21 @@
         where = (1 - core) if b == 0 else core
         start = pl.multiple_of((c * CORES + where) * size + h * half, half)
         return pltpu.make_async_copy(
-            pre.at[pl.ds(start, half)], pre_buf.at[j % 2, pl.ds(b * half, half)], pre_sem.at[j % 2, b]
+            pre.at[pl.ds(start, half)], pre_buf.at[j % 2, pl.ds(b * half, half)], pre_sem.at[j % 2]
         )
 
     def pair_sum(j):
-        return remote(st_pair.at[pl.ds(pl.multiple_of(j % 2 * half, half), half)], pair_buf.at[j % 2], rsp_s.at[j], rsp_r.at[j], partner)
+        return remote(st_pair.at[pl.ds(pl.multiple_of(j % 2 * half, half), half)], pair_buf.at[j % 2], rsp_s.at[j % 2], rsp_r.at[j % 2], partner)
 
     def ring_sum(j):
         dev = lax.rem(me + n - CORES + 2 * CORES * (j % 2), n)
-        return remote(st_ring.at[j - 4], ring_buf.at[j - 4], rsg_s.at[j - 4], rsg_r.at[j - 4], dev)
+        return remote(st_ring.at[j - 4], ring_buf.at[j - 4], sum_s.at[j - 4 - (j - 4) // 3], rsg_r.at[j - 4], dev)
+
+    pieces = ((0, half - LAST), (half - LAST, LAST))
 
     def chain_send(b, q):
-        ref = (b, pl.ds(q * piece, piece))
-        return remote(st_ring.at[ref], chain_buf.at[ref], ch_s.at[b, q], ch_r.at[b, q], left if b == 0 else right)
+        ref = (b, pl.ds(*pieces[q]))
+        return remote(st_ring.at[ref], chain_buf.at[ref], sum_s.at[2], ch_r.at[b, q], left if b == 0 else right)
 
     barrier = pltpu.get_barrier_semaphore()
     for dev in (left, right, partner):
@@ -173,6 +167,7 @@
     def _(r):
         acc_in[pl.ds(pl.multiple_of(r, 128), 128)] = jnp.zeros((128, ff), F32)
 
+    start_rows(DY, 0)
     pltpu.make_async_copy(w_down, wd, w_sem.at[0]).wait()
     pltpu.make_async_copy(w_in, wi, w_sem.at[1]).wait()
 
@@ -182,7 +177,7 @@
     def _(i):
         slot = i % 2
 
-        @pl.when(i == 2)
+        @pl.when(i == 1)
         def _():
             service(DY, 2)
             service(DY, 3)
@@ -191,26 +186,26 @@
             to_partner(X, 0).start()
             to_partner(X, 1).start()
 
-        @pl.when(i == 4)
+        @pl.when(i == 3)
         def _():
             service(DY, 4)
             service(DY, 5)
             ring_own(X, 4).start()
             ring_own(X, 5).start()
 
-        @pl.when(i == 6)
+        @pl.when(i == 5)
         def _():
             service(DY, 6)
             service(DY, 7)
 
         @pl.when(i < PAIRS - 1)
         def _():
+            start_rows(DY, i + 1)
             for b in range(2):
                 pre_load(i + 1, b).start()
 
-        rows = rows_of(DY, i)
-        for b in range(2):
-            pre_load(i, b).wait()
+        rows = rows_of(i)
+        pltpu.make_async_copy(pre_buf.at[slot], pre_buf.at[slot], pre_sem.at[slot]).wait()
 
         @pl.loop(0, ff, step=tile)
         def _(f):
@@ -266,7 +261,7 @@
 
     service(X, 2)
     service(X, 3)
-
+    start_rows(X, 0)
     for b in range(2):
         pair_sum(PAIRS - 2 + b).wait_send()
 
@@ -284,7 +279,7 @@
             rs = pl.ds(pl.multiple_of(r, 32), 32)
             st_ring[b, rs] = (stash[2 + b, rs] + ring_buf[2 + b, rs].astype(F32)).astype(BF16)
 
-        for q in range(PIECES):
+        for q in range(len(pieces)):
             chain_send(b, q).start()
 
     def direct(b):
@@ -297,21 +292,27 @@
 
     @pl.loop(0, PAIRS)
     def _(i):
-        @pl.when(i == 4)
+        @pl.when(i == 3)
+        def _():
+            service(X, 4)
+            service(X, 5)
+
+        @pl.when(i == PAIRS - 2)
         def _():
             direct(0)
             direct(1)
             chain(0)
             chain(1)
-            service(X, 4)
-            service(X, 5)
-
-        @pl.when(i == 6)
-        def _():
             service(X, 6)
             service(X, 7)
-
-        rows = rows_of(X, i)
+            start_rows(X, i)
+            start_rows(X, i + 1)
+
+        @pl.when(i < PAIRS - 3)
+        def _():
+            start_rows(X, i + 1)
+
+        rows = rows_of(i)
 
         @pl.loop(0, d, step=tile)
         def _(c):
@@ -327,38 +328,33 @@
         rs = pl.ds(pl.multiple_of(r, 64), 64)
         dw_in[rs] = acc_in[rs].astype(BF16)
 
-    for w in (DY, X):
-        for j in range(2, PAIRS):
-            ring_send(w, j).wait_send()
-        for j in range(PAIRS):
-            to_partner(w, j).wait_send()
-    for j in (6, 7):
-        ring_sum(j).wait_send()
-
-    for q in range(PIECES):
+    ring_sent = x_all.at[pl.ds(0, PAIRS - 2)]
+    remote(ring_sent, ring_sent, ring_s.at[0], ring_r.at[0, 0], right).wait_send()
+    remote(x_all, x_all, pair_s.at[0], pair_r.at[0], partner).wait_send()
+
+    for q in range(len(pieces)):
         for b in range(2):
             chain_send(b, q).wait_recv()
-            rs = pl.ds(q * piece, piece)
-            dx[pl.ds(b * half + q * piece, piece)] = (stash[b, rs] + chain_buf[b, rs].astype(F32)).astype(BF16)
-
-    for b in range(2):
-        for q in range(PIECES):
-            chain_send(b, q).wait_send()
+
+            @pl.loop(0, pieces[q][1], step=LAST)
+            def _(r):
+                rs = pl.ds(pl.multiple_of(pieces[q][0] + r, LAST), LAST)
+                to = pl.ds(pl.multiple_of(b * half + pieces[q][0] + r, LAST), LAST)
+                dx[to] = (stash[b, rs] + chain_buf[b, rs].astype(F32)).astype(BF16)
+
+    remote(st_ring, ring_buf, sum_s.at[2], rsg_r.at[0], left).wait_send()
 
 
 def results(*refs):
     count = len(refs) // 2
     ins, outs, sem = refs[:count], refs[count : 2 * count], refs[-1]
-    copies = []
-    for a, b in zip(ins, outs):
+    for i, (a, b) in enumerate(zip(ins, outs)):
         rows = a.shape[0] // 2
-        for i in range(2):
-            rs = pl.ds(i * rows, rows)
-            copies.append(pltpu.make_async_copy(a.at[rs], b.at[rs], sem.at[len(copies)]))
-    for c in copies:
-        c.start()
-    for c in copies:
-        c.wait()
+        for start in (0, rows):
+            rs = pl.ds(start, rows)
+            pltpu.make_async_copy(a.at[rs], b.at[rs], sem.at[i]).start()
+    for i, (a, b) in enumerate(zip(ins, outs)):
+        pltpu.make_async_copy(a, b, sem.at[i]).wait()
 
 
 def solution(mesh):
@@ -391,9 +387,8 @@
                 pltpu.VMEM((2, half, d), BF16),
                 pltpu.VMEM((4, half, d), BF16),
                 pltpu.VMEM((2, half, d), BF16),
-                dma((2, PAIRS)), dma((2, PAIRS)), dma((2, PAIRS)), dma((2, PAIRS)),
-                dma((PAIRS,)), dma((PAIRS,)), dma((4,)), dma((4,)), dma((2, PIECES)), dma((2, PIECES)),
-                dma((2,)), dma((2, 2)), dma((2, 2)),
+                dma((1,)), dma((2, PAIRS - 2)), dma((1,)), dma((PAIRS,)), dma((2,)), dma((2,)), dma((3,)), dma((4,)),
+                dma((2, 2)), dma((2,)), dma((2,)), dma((2,)),
             ],
             compiler_params=pltpu.CompilerParams(collective_id=0, has_side_effects=True, vmem_limit_bytes=VMEM_LIMIT),
             name="mlp_backward",
@@ -404,7 +399,7 @@
                 out_shape=[jax.ShapeDtypeStruct(s, BF16) for s in shapes],
                 in_specs=[pl.BlockSpec(memory_space=pltpu.VMEM)] * 3,
                 out_specs=[any_space] * 3,
-                scratch_shapes=[dma((6,))],
+                scratch_shapes=[dma((3,))],
                 compiler_params=pltpu.CompilerParams(vmem_limit_bytes=2**20),
                 name="results",
             )(*(pltpu.with_memory_space_constraint(o, pltpu.VMEM) for o in outs[:3]))

time: 213 us -> 213 us (level)
  no operation moved by 1% of the time
where the time goes in v3:
time: 213 us
  Pallas kernels  212 us (100%)
    pallas_call x1, Pallas kernels, step(): pl.pallas_call(functools.partial(kernel, n), out_shape=[pltpu.VMEM(s, BF1...  208 us

profile of v3, /device:TPU:112, one launch (start us, length us, event | category | flops | bytes accessed | tf_op | source)
XLA Modules:
  0.0 212.6 jit_solution(3903975042530943610)
XLA Ops:
  0.6 208.0 %mlp_backward.1 = (bf16[512,2048]{1,0:T(8,128)(2,1)S(1)}, bf16[2048,1024]{1,0:T(8,128)(2,1)S(1)}, bf16[1024,2048]{1,0:T(8,128)(2,1)S(1)}, bf16[8,512,2048]{2,1,0:T(8,128)(2,1)}, bf16[8,512,2048]{2,1,0:T(8,128)(2,1)}) custom-call(bf16[512,2048]{1,0:T(8,128)(2,1)} %x.1, bf16[512,2048]{1,0:T(8,128)(2,1)} %dy.1, bf16[4096,1024]{1,0:T(8,128)(2,1)} %pre.1, ...), custom_call_target="tpu_custom_call" | custom-call | tf_op jit(solution)/shard_map/mlp_backward/pallas_call | solution.py:369
  208.6 4.0 %results.1 = (bf16[512,2048]{1,0:T(8,128)(2,1)}, bf16[2048,1024]{1,0:T(8,128)(2,1)}, bf16[1024,2048]{1,0:T(8,128)(2,1)}) custom-call(bf16[512,2048]{1,0:T(8,128)(2,1)S(1)} %get-tuple-element.6.refs_0_, bf16[2048,1024]{1,0:T(8,128)(2,1)S(1)} %get-tuple-element.7.refs_1_, bf16[1024,2048]{1,0:T(8,128)(2,1)S(1)} %get-tuple-element.8.refs_2_), custom_call_target="tpu_custom_call" | custom-call | tf_op jit(solution)/shard_map/results/pallas_call | solution.py:397

commit v4 on v3

--- a/solution.py
+++ b/solution.py
@@ -31,7 +31,7 @@
     n, x, dy, pre, w_in, w_down,
     dx, dw_in, dw_down, x_all, dy_all,
     acc_in, acc_down, dpre, stash, st_ring, rows_buf, pre_buf, hid, pair_buf, ring_buf, chain_buf,
-    ring_s, ring_r, pair_s, pair_r, rsp_s, rsp_r, sum_s, rsg_r, ch_r, w_sem, pre_sem, ld_sem,
+    ring_s, ring_r, pair_s, pair_r, rsp_s, rsp_r, sum_s, sum_r, ch_r, w_sem, pre_sem, ld_sem,
 ):
     wi, wd, st_pair = dw_in, dw_down, dx
     me = lax.axis_index("tp")
@@ -72,32 +72,26 @@
 
     def ring_own(w, j):
         h = {2: 0, 3: 1, 4: 1, 5: 0}[j]
-        return remote(own_half(w, h), at(gathered[w], me, h), ring_s.at[0], ring_r.at[w, j - 2], right if j % 2 == 0 else left)
+        return remote(own_half(w, h), at(gathered[w], me, h), ring_s.at[0], ring_r.at[w, j // 2 - 1], right if j % 2 == 0 else left)
 
     def ring_relay(w, j):
         ref = of_core(gathered[w], j - 4, core)
-        return remote(ref, ref, ring_s.at[0], ring_r.at[w, j - 2], right if j % 2 == 0 else left)
+        return remote(ref, ref, ring_s.at[0], ring_r.at[w, j // 2 - 1], right if j % 2 == 0 else left)
 
     def ring_send(w, j):
         return ring_own(w, j) if j < 6 else ring_relay(w, j)
 
-    def ring_got(w, j):
-        ref = of_core(gathered[w], j, core)
-        return remote(ref, ref, ring_s.at[0], ring_r.at[w, j - 2], right)
-
     def to_partner(w, j):
         src = own_half(w, j) if j < 2 else of_core(gathered[w], j, core)
-        return remote(src, of_core(gathered[w], j, core), pair_s.at[0], pair_r.at[j], partner)
-
-    def from_partner(w, j):
-        ref = of_core(gathered[w], j, 1 - core)
-        return remote(ref, ref, pair_s.at[0], pair_r.at[j], partner)
+        return remote(src, of_core(gathered[w], j, core), pair_s.at[0], pair_r.at[j // 2], partner)
 
     def service(w, j):
-        ring_got(w, j).wait_recv()
-        if j < 4:
-            ring_relay(w, j + 4).start()
-        to_partner(w, j).start()
+        both = gathered[w].at[0]
+        remote(both, both, ring_s.at[0], ring_r.at[w, j // 2 - 1], right).wait_recv()
+        for q in (j, j + 1):
+            if q < 4:
+                ring_relay(w, q + 4).start()
+            to_partner(w, q).start()
 
     def load(src, dst, sem):
         c = pltpu.make_async_copy(src, dst, sem)
@@ -105,7 +99,11 @@
         return c
 
     def start_rows(w, j):
-        from_partner(w, j).wait_recv()
+        @pl.when(j % 2 == 0)
+        def _():
+            both = gathered[w].at[0]
+            remote(both, both, pair_s.at[0], pair_r.at[j // 2], partner).wait_recv()
+
         slot = j % 2
         load(of_core(gathered[w], j, 1 - core), rows_buf.at[slot, pl.ds(0, half)], ld_sem.at[slot])
         c, h = place(j)
@@ -137,13 +135,13 @@
 
     def ring_sum(j):
         dev = lax.rem(me + n - CORES + 2 * CORES * (j % 2), n)
-        return remote(st_ring.at[j - 4], ring_buf.at[j - 4], sum_s.at[j - 4 - (j - 4) // 3], rsg_r.at[j - 4], dev)
+        return remote(st_ring.at[j - 4], ring_buf.at[j - 4], sum_s.at[j // 2 - 2], sum_r.at[j // 2 - 2], dev)
 
     pieces = ((0, half - LAST), (half - LAST, LAST))
 
     def chain_send(b, q):
         ref = (b, pl.ds(*pieces[q]))
-        return remote(st_ring.at[ref], chain_buf.at[ref], sum_s.at[2], ch_r.at[b, q], left if b == 0 else right)
+        return remote(st_ring.at[ref], chain_buf.at[ref], sum_s.at[1], ch_r.at[q], left if b == 0 else right)
 
     barrier = pltpu.get_barrier_semaphore()
     for dev in (left, right, partner):
@@ -180,7 +178,6 @@
         @pl.when(i == 1)
         def _():
             service(DY, 2)
-            service(DY, 3)
             ring_own(X, 2).start()
             ring_own(X, 3).start()
             to_partner(X, 0).start()
@@ -189,14 +186,12 @@
         @pl.when(i == 3)
         def _():
             service(DY, 4)
-            service(DY, 5)
             ring_own(X, 4).start()
             ring_own(X, 5).start()
 
         @pl.when(i == 5)
         def _():
             service(DY, 6)
-            service(DY, 7)
 
         @pl.when(i < PAIRS - 1)
         def _():
@@ -260,7 +255,6 @@
             ring_sum(i).start()
 
     service(X, 2)
-    service(X, 3)
     start_rows(X, 0)
     for b in range(2):
         pair_sum(PAIRS - 2 + b).wait_send()
@@ -270,10 +264,11 @@
         rs = pl.ds(pl.multiple_of(r, 32), 32)
         dw_down[rs] = acc_down[rs].astype(BF16)
 
+    def hops(q):
+        both = pl.ds(2 * q, 2)
+        return remote(st_ring.at[both], ring_buf.at[both], sum_s.at[q], sum_r.at[q], right)
+
     def chain(b):
-        ring_sum(6 + b).wait_recv()
-        ring_sum(4 + b).wait_send()
-
         @pl.loop(0, half, step=32)
         def _(r):
             rs = pl.ds(pl.multiple_of(r, 32), 32)
@@ -283,8 +278,6 @@
             chain_send(b, q).start()
 
     def direct(b):
-        ring_sum(4 + b).wait_recv()
-
         @pl.loop(0, half, step=32)
         def _(r):
             rs = pl.ds(pl.multiple_of(r, 32), 32)
@@ -295,16 +288,16 @@
         @pl.when(i == 3)
         def _():
             service(X, 4)
-            service(X, 5)
 
         @pl.when(i == PAIRS - 2)
         def _():
+            hops(0).wait()
             direct(0)
             direct(1)
+            hops(1).wait_recv()
             chain(0)
             chain(1)
             service(X, 6)
-            service(X, 7)
             start_rows(X, i)
             start_rows(X, i + 1)
 
@@ -333,8 +326,9 @@
     remote(x_all, x_all, pair_s.at[0], pair_r.at[0], partner).wait_send()
 
     for q in range(len(pieces)):
+        both = chain_buf.at[:, pl.ds(*pieces[q])]
+        remote(both, both, sum_s.at[1], ch_r.at[q], right).wait_recv()
         for b in range(2):
-            chain_send(b, q).wait_recv()
 
             @pl.loop(0, pieces[q][1], step=LAST)
             def _(r):
@@ -342,15 +336,15 @@
                 to = pl.ds(pl.multiple_of(b * half + pieces[q][0] + r, LAST), LAST)
                 dx[to] = (stash[b, rs] + chain_buf[b, rs].astype(F32)).astype(BF16)
 
-    remote(st_ring, ring_buf, sum_s.at[2], rsg_r.at[0], left).wait_send()
+    remote(st_ring, ring_buf, sum_s.at[1], sum_r.at[1], left).wait_send()
 
 
 def results(*refs):
     count = len(refs) // 2
     ins, outs, sem = refs[:count], refs[count : 2 * count], refs[-1]
     for i, (a, b) in enumerate(zip(ins, outs)):
-        rows = a.shape[0] // 2
-        for start in (0, rows):
+        rows = a.shape[0] // 8
+        for start in range(0, a.shape[0], rows):
             rs = pl.ds(start, rows)
             pltpu.make_async_copy(a.at[rs], b.at[rs], sem.at[i]).start()
     for i, (a, b) in enumerate(zip(ins, outs)):
@@ -387,8 +381,8 @@
                 pltpu.VMEM((2, half, d), BF16),
                 pltpu.VMEM((4, half, d), BF16),
                 pltpu.VMEM((2, half, d), BF16),
-                dma((1,)), dma((2, PAIRS - 2)), dma((1,)), dma((PAIRS,)), dma((2,)), dma((2,)), dma((3,)), dma((4,)),
-                dma((2, 2)), dma((2,)), dma((2,)), dma((2,)),
+                dma((1,)), dma((2, 3)), dma((1,)), dma((PAIRS // 2,)), dma((2,)), dma((2,)), dma((2,)), dma((2,)),
+                dma((2,)), dma((2,)), dma((2,)), dma((2,)),
             ],
             compiler_params=pltpu.CompilerParams(collective_id=0, has_side_effects=True, vmem_limit_bytes=VMEM_LIMIT),
             name="mlp_backward",

time: 213 us -> 213 us (level)
  no operation moved by 1% of the time
where the time goes in v4:
time: 213 us; the launch traced here: 212 us
  Pallas kernels  212 us (100%)
    pallas_call x1, Pallas kernels, step(): pl.pallas_call(functools.partial(kernel, n), out_shape=[pltpu.VMEM(s, BF1...  208 us

profile of v4, /device:TPU:112, one launch (start us, length us, event | category | flops | bytes accessed | tf_op | source)
XLA Modules:
  0.0 212.4 jit_solution(12676135668068383190)
XLA Ops:
  0.6 207.9 %mlp_backward.1 = (bf16[512,2048]{1,0:T(8,128)(2,1)S(1)}, bf16[2048,1024]{1,0:T(8,128)(2,1)S(1)}, bf16[1024,2048]{1,0:T(8,128)(2,1)S(1)}, bf16[8,512,2048]{2,1,0:T(8,128)(2,1)}, bf16[8,512,2048]{2,1,0:T(8,128)(2,1)}) custom-call(bf16[512,2048]{1,0:T(8,128)(2,1)} %x.1, bf16[512,2048]{1,0:T(8,128)(2,1)} %dy.1, bf16[4096,1024]{1,0:T(8,128)(2,1)} %pre.1, ...), custom_call_target="tpu_custom_call" | custom-call | tf_op jit(solution)/shard_map/mlp_backward/pallas_call | solution.py:363
  208.5 3.9 %results.1 = (bf16[512,2048]{1,0:T(8,128)(2,1)}, bf16[2048,1024]{1,0:T(8,128)(2,1)}, bf16[1024,2048]{1,0:T(8,128)(2,1)}) custom-call(bf16[512,2048]{1,0:T(8,128)(2,1)S(1)} %get-tuple-element.6.refs_0_, bf16[2048,1024]{1,0:T(8,128)(2,1)S(1)} %get-tuple-element.7.refs_1_, bf16[1024,2048]{1,0:T(8,128)(2,1)S(1)} %get-tuple-element.8.refs_2_), custom_call_target="tpu_custom_call" | custom-call | tf_op jit(solution)/shard_map/results/pallas_call | solution.py:391

commit v5 on v4

--- a/solution.py
+++ b/solution.py
@@ -11,7 +11,8 @@
 F32, BF16 = jnp.float32, jnp.bfloat16
 CORES = 2
 PAIRS = 8
-LAST = 32
+LAST = 16
+ROWS = 8
 NT = (((1,), (1,)), ((), ()))
 TN = (((0,), (0,)), ((), ()))
 DY, X = 0, 1
@@ -342,13 +343,12 @@
 def results(*refs):
     count = len(refs) // 2
     ins, outs, sem = refs[:count], refs[count : 2 * count], refs[-1]
-    for i, (a, b) in enumerate(zip(ins, outs)):
-        rows = a.shape[0] // 8
-        for start in range(0, a.shape[0], rows):
-            rs = pl.ds(start, rows)
-            pltpu.make_async_copy(a.at[rs], b.at[rs], sem.at[i]).start()
-    for i, (a, b) in enumerate(zip(ins, outs)):
-        pltpu.make_async_copy(a, b, sem.at[i]).wait()
+    for a, b in zip(ins, outs):
+        for start in range(0, a.shape[0], ROWS):
+            rs = pl.ds(start, ROWS)
+            pltpu.make_async_copy(a.at[rs], b.at[rs], sem.at[0]).start()
+    for a, b in zip(ins, outs):
+        pltpu.make_async_copy(a, b, sem.at[0]).wait()
 
 
 def solution(mesh):
@@ -393,7 +393,7 @@
                 out_shape=[jax.ShapeDtypeStruct(s, BF16) for s in shapes],
                 in_specs=[pl.BlockSpec(memory_space=pltpu.VMEM)] * 3,
                 out_specs=[any_space] * 3,
-                scratch_shapes=[dma((3,))],
+                scratch_shapes=[dma((1,))],
                 compiler_params=pltpu.CompilerParams(vmem_limit_bytes=2**20),
                 name="results",
             )(*(pltpu.with_memory_space_constraint(o, pltpu.VMEM) for o in outs[:3]))

time: 213 us -> 212 us (level)
  no operation moved by 1% of the time
where the time goes in v5:
time: 212 us
  Pallas kernels  212 us (100%)
    pallas_call x1, Pallas kernels, step(): pl.pallas_call(functools.partial(kernel, n), out_shape=[pltpu.VMEM(s, BF1...  208 us

profile of v5, /device:TPU:112, one launch (start us, length us, event | category | flops | bytes accessed | tf_op | source)
XLA Modules:
  0.0 212.3 jit_solution(15415952447308456879)
XLA Ops:
  0.6 207.8 %mlp_backward.1 = (bf16[512,2048]{1,0:T(8,128)(2,1)S(1)}, bf16[2048,1024]{1,0:T(8,128)(2,1)S(1)}, bf16[1024,2048]{1,0:T(8,128)(2,1)S(1)}, bf16[8,512,2048]{2,1,0:T(8,128)(2,1)}, bf16[8,512,2048]{2,1,0:T(8,128)(2,1)}) custom-call(bf16[512,2048]{1,0:T(8,128)(2,1)} %x.1, bf16[512,2048]{1,0:T(8,128)(2,1)} %dy.1, bf16[4096,1024]{1,0:T(8,128)(2,1)} %pre.1, ...), custom_call_target="tpu_custom_call" | custom-call | tf_op jit(solution)/shard_map/mlp_backward/pallas_call | solution.py:363
  208.5 3.8 %results.1 = (bf16[512,2048]{1,0:T(8,128)(2,1)}, bf16[2048,1024]{1,0:T(8,128)(2,1)}, bf16[1024,2048]{1,0:T(8,128)(2,1)}) custom-call(bf16[512,2048]{1,0:T(8,128)(2,1)S(1)} %get-tuple-element.6.refs_0_, bf16[2048,1024]{1,0:T(8,128)(2,1)S(1)} %get-tuple-element.7.refs_1_, bf16[1024,2048]{1,0:T(8,128)(2,1)S(1)} %get-tuple-element.8.refs_2_), custom_call_target="tpu_custom_call" | custom-call | tf_op jit(solution)/shard_map/results/pallas_call | solution.py:391

commit v6 on v5

--- a/solution.py
+++ b/solution.py
@@ -32,7 +32,7 @@
     n, x, dy, pre, w_in, w_down,
     dx, dw_in, dw_down, x_all, dy_all,
     acc_in, acc_down, dpre, stash, st_ring, rows_buf, pre_buf, hid, pair_buf, ring_buf, chain_buf,
-    ring_s, ring_r, pair_s, pair_r, rsp_s, rsp_r, sum_s, sum_r, ch_r, w_sem, pre_sem, ld_sem,
+    sent, ring_r, pair_r, rsp_s, rsp_r, sum_r, ch_r, ld_sem,
 ):
     wi, wd, st_pair = dw_in, dw_down, dx
     me = lax.axis_index("tp")
@@ -71,25 +71,32 @@
             src_ref=src, dst_ref=dst, send_sem=s, recv_sem=r, device_id={"tp": dev}, device_id_type=MESH
         )
 
+    def ring_sem(w, j):
+        return ring_r.at[j // 2 - 1 if w == DY else 3 + j // 6]
+
+    def pair_sem(j):
+        return pair_r.at[(j // 2 + 1) // 2]
+
     def ring_own(w, j):
         h = {2: 0, 3: 1, 4: 1, 5: 0}[j]
-        return remote(own_half(w, h), at(gathered[w], me, h), ring_s.at[0], ring_r.at[w, j // 2 - 1], right if j % 2 == 0 else left)
+        return remote(own_half(w, h), at(gathered[w], me, h), sent.at[0], ring_sem(w, j), right if j % 2 == 0 else left)
 
     def ring_relay(w, j):
         ref = of_core(gathered[w], j - 4, core)
-        return remote(ref, ref, ring_s.at[0], ring_r.at[w, j // 2 - 1], right if j % 2 == 0 else left)
+        return remote(ref, ref, sent.at[0], ring_sem(w, j), right if j % 2 == 0 else left)
 
     def ring_send(w, j):
         return ring_own(w, j) if j < 6 else ring_relay(w, j)
 
     def to_partner(w, j):
         src = own_half(w, j) if j < 2 else of_core(gathered[w], j, core)
-        return remote(src, of_core(gathered[w], j, core), pair_s.at[0], pair_r.at[j // 2], partner)
+        return remote(src, of_core(gathered[w], j, core), sent.at[0], pair_sem(j), partner)
 
     def service(w, j):
-        both = gathered[w].at[0]
-        remote(both, both, ring_s.at[0], ring_r.at[w, j // 2 - 1], right).wait_recv()
-        for q in (j, j + 1):
+        count = 4 if w == X and j == 2 else 2
+        some = gathered[w].at[pl.ds(0, count // 2)]
+        remote(some, some, sent.at[0], ring_sem(w, j), right).wait_recv()
+        for q in range(j, j + count):
             if q < 4:
                 ring_relay(w, q + 4).start()
             to_partner(w, q).start()
@@ -100,10 +107,15 @@
         return c
 
     def start_rows(w, j):
-        @pl.when(j % 2 == 0)
-        def _():
-            both = gathered[w].at[0]
-            remote(both, both, pair_s.at[0], pair_r.at[j // 2], partner).wait_recv()
+        def arrived(pairs):
+            some = gathered[w].at[pl.ds(0, pairs // 2)]
+            remote(some, some, sent.at[0], pair_sem(j), partner).wait_recv()
+
+        if w == DY:
+            pl.when(j % 2 == 0)(lambda: arrived(2))
+        else:
+            for first, pairs in ((0, 2), (2, 4), (6, 2)):
+                pl.when(j == first)(functools.partial(arrived, pairs))
 
         slot = j % 2
         load(of_core(gathered[w], j, 1 - core), rows_buf.at[slot, pl.ds(0, half)], ld_sem.at[slot])
@@ -128,21 +140,21 @@
         where = (1 - core) if b == 0 else core
         start = pl.multiple_of((c * CORES + where) * size + h * half, half)
         return pltpu.make_async_copy(
-            pre.at[pl.ds(start, half)], pre_buf.at[j % 2, pl.ds(b * half, half)], pre_sem.at[j % 2]
+            pre.at[pl.ds(start, half)], pre_buf.at[j % 2, pl.ds(b * half, half)], ld_sem.at[j % 2]
         )
 
     def pair_sum(j):
-        return remote(st_pair.at[pl.ds(pl.multiple_of(j % 2 * half, half), half)], pair_buf.at[j % 2], rsp_s.at[j % 2], rsp_r.at[j % 2], partner)
+        return remote(st_pair.at[pl.ds(pl.multiple_of(j % 2 * half, half), half)], pair_buf.at[j % 2], rsp_s.at[0], rsp_r.at[j % 2], partner)
 
     def ring_sum(j):
         dev = lax.rem(me + n - CORES + 2 * CORES * (j % 2), n)
-        return remote(st_ring.at[j - 4], ring_buf.at[j - 4], sum_s.at[j // 2 - 2], sum_r.at[j // 2 - 2], dev)
+        return remote(st_ring.at[j - 4], ring_buf.at[j - 4], sent.at[3 - j // 2], sum_r.at[0], dev)
 
     pieces = ((0, half - LAST), (half - LAST, LAST))
 
     def chain_send(b, q):
         ref = (b, pl.ds(*pieces[q]))
-        return remote(st_ring.at[ref], chain_buf.at[ref], sum_s.at[1], ch_r.at[q], left if b == 0 else right)
+        return remote(st_ring.at[ref], chain_buf.at[ref], sent.at[0], ch_r.at[q], left if b == 0 else right)
 
     barrier = pltpu.get_barrier_semaphore()
     for dev in (left, right, partner):
@@ -155,8 +167,8 @@
         to_partner(DY, j).start()
     for b in range(2):
         pre_load(0, b).start()
-    load(w_down, wd, w_sem.at[0])
-    load(w_in, wi, w_sem.at[1])
+    load(w_down, wd, ld_sem.at[1])
+    load(w_in, wi, ld_sem.at[1])
 
     @pl.loop(0, ff, step=64)
     def _(r):
@@ -167,8 +179,8 @@
         acc_in[pl.ds(pl.multiple_of(r, 128), 128)] = jnp.zeros((128, ff), F32)
 
     start_rows(DY, 0)
-    pltpu.make_async_copy(w_down, wd, w_sem.at[0]).wait()
-    pltpu.make_async_copy(w_in, wi, w_sem.at[1]).wait()
+    pltpu.make_async_copy(w_down, wd, ld_sem.at[1]).wait()
+    pltpu.make_async_copy(w_in, wi, ld_sem.at[1]).wait()
 
     tile = 256
 
@@ -201,7 +213,7 @@
                 pre_load(i + 1, b).start()
 
         rows = rows_of(i)
-        pltpu.make_async_copy(pre_buf.at[slot], pre_buf.at[slot], pre_sem.at[slot]).wait()
+        pltpu.make_async_copy(pre_buf.at[slot], pre_buf.at[slot], ld_sem.at[slot]).wait()
 
         @pl.loop(0, ff, step=tile)
         def _(f):
@@ -211,9 +223,9 @@
             dpre[i, :, fs] = (dh * slope).astype(BF16)
             hid[:, fs] = h.astype(BF16)
 
-        @pl.when(i >= 2)
-        def _():
-            pair_sum(i - 2).wait_send()
+        @pl.when(i >= 1)
+        def _():
+            pair_sum(i - 1).wait_send()
 
         @pl.loop(0, d, step=2 * tile)
         def _(c):
@@ -257,17 +269,12 @@
 
     service(X, 2)
     start_rows(X, 0)
-    for b in range(2):
-        pair_sum(PAIRS - 2 + b).wait_send()
+    pair_sum(PAIRS - 1).wait_send()
 
     @pl.loop(0, ff, step=32)
     def _(r):
         rs = pl.ds(pl.multiple_of(r, 32), 32)
         dw_down[rs] = acc_down[rs].astype(BF16)
-
-    def hops(q):
-        both = pl.ds(2 * q, 2)
-        return remote(st_ring.at[both], ring_buf.at[both], sum_s.at[q], sum_r.at[q], right)
 
     def chain(b):
         @pl.loop(0, half, step=32)
@@ -286,16 +293,13 @@
 
     @pl.loop(0, PAIRS)
     def _(i):
-        @pl.when(i == 3)
-        def _():
-            service(X, 4)
-
         @pl.when(i == PAIRS - 2)
         def _():
-            hops(0).wait()
+            remote(st_ring, ring_buf, sent.at[0], sum_r.at[0], right).wait_recv()
+            near = pl.ds(0, 2)
+            remote(st_ring.at[near], ring_buf.at[near], sent.at[1], sum_r.at[0], right).wait_send()
             direct(0)
             direct(1)
-            hops(1).wait_recv()
             chain(0)
             chain(1)
             service(X, 6)
@@ -322,13 +326,9 @@
         rs = pl.ds(pl.multiple_of(r, 64), 64)
         dw_in[rs] = acc_in[rs].astype(BF16)
 
-    ring_sent = x_all.at[pl.ds(0, PAIRS - 2)]
-    remote(ring_sent, ring_sent, ring_s.at[0], ring_r.at[0, 0], right).wait_send()
-    remote(x_all, x_all, pair_s.at[0], pair_r.at[0], partner).wait_send()
-
     for q in range(len(pieces)):
         both = chain_buf.at[:, pl.ds(*pieces[q])]
-        remote(both, both, sum_s.at[1], ch_r.at[q], right).wait_recv()
+        remote(both, both, sent.at[0], ch_r.at[q], right).wait_recv()
         for b in range(2):
 
             @pl.loop(0, pieces[q][1], step=LAST)
@@ -337,16 +337,17 @@
                 to = pl.ds(pl.multiple_of(b * half + pieces[q][0] + r, LAST), LAST)
                 dx[to] = (stash[b, rs] + chain_buf[b, rs].astype(F32)).astype(BF16)
 
-    remote(st_ring, ring_buf, sum_s.at[1], sum_r.at[1], left).wait_send()
+    for some in (x_all.at[pl.ds(0, PAIRS - 2)], x_all, st_ring):
+        remote(some, some, sent.at[0], sum_r.at[0], right).wait_send()
 
 
 def results(*refs):
     count = len(refs) // 2
     ins, outs, sem = refs[:count], refs[count : 2 * count], refs[-1]
-    for a, b in zip(ins, outs):
-        for start in range(0, a.shape[0], ROWS):
-            rs = pl.ds(start, ROWS)
-            pltpu.make_async_copy(a.at[rs], b.at[rs], sem.at[0]).start()
+    todo = [(a, b, start) for a, b in zip(ins, outs) for start in range(0, a.shape[0], ROWS)]
+    for a, b, start in sorted(todo, key=lambda t: t[2] / t[0].shape[0]):
+        rs = pl.ds(start, ROWS)
+        pltpu.make_async_copy(a.at[rs], b.at[rs], sem.at[0]).start()
     for a, b in zip(ins, outs):
         pltpu.make_async_copy(a, b, sem.at[0]).wait()
 
@@ -381,8 +382,7 @@
                 pltpu.VMEM((2, half, d), BF16),
                 pltpu.VMEM((4, half, d), BF16),
                 pltpu.VMEM((2, half, d), BF16),
-                dma((1,)), dma((2, 3)), dma((1,)), dma((PAIRS // 2,)), dma((2,)), dma((2,)), dma((2,)), dma((2,)),
-                dma((2,)), dma((2,)), dma((2,)), dma((2,)),
+                dma((2,)), dma((5,)), dma((3,)), dma((1,)), dma((2,)), dma((1,)), dma((2,)), dma((2,)),
             ],
             compiler_params=pltpu.CompilerParams(collective_id=0, has_side_effects=True, vmem_limit_bytes=VMEM_LIMIT),
             name="mlp_backward",

time: 212 us -> 212 us (level)
  no operation moved by 1% of the time
where the time goes in v6:
time: 212 us
  Pallas kernels  212 us (100%)
    pallas_call x1, Pallas kernels, step(): pl.pallas_call(functools.partial(kernel, n), out_shape=[pltpu.VMEM(s, BF1...  208 us

profile of v6, /device:TPU:112, one launch (start us, length us, event | category | flops | bytes accessed | tf_op | source)
XLA Modules:
  0.0 212.2 jit_solution(2223527903669969275)
XLA Ops:
  0.6 207.7 %mlp_backward.1 = (bf16[512,2048]{1,0:T(8,128)(2,1)S(1)}, bf16[2048,1024]{1,0:T(8,128)(2,1)S(1)}, bf16[1024,2048]{1,0:T(8,128)(2,1)S(1)}, bf16[8,512,2048]{2,1,0:T(8,128)(2,1)}, bf16[8,512,2048]{2,1,0:T(8,128)(2,1)}) custom-call(bf16[512,2048]{1,0:T(8,128)(2,1)} %x.1, bf16[512,2048]{1,0:T(8,128)(2,1)} %dy.1, bf16[4096,1024]{1,0:T(8,128)(2,1)} %pre.1, ...), custom_call_target="tpu_custom_call" | custom-call | tf_op jit(solution)/shard_map/mlp_backward/pallas_call | solution.py:364
  208.4 3.8 %results.1 = (bf16[512,2048]{1,0:T(8,128)(2,1)}, bf16[2048,1024]{1,0:T(8,128)(2,1)}, bf16[1024,2048]{1,0:T(8,128)(2,1)}) custom-call(bf16[512,2048]{1,0:T(8,128)(2,1)S(1)} %get-tuple-element.6.refs_0_, bf16[2048,1024]{1,0:T(8,128)(2,1)S(1)} %get-tuple-element.7.refs_1_, bf16[1024,2048]{1,0:T(8,128)(2,1)S(1)} %get-tuple-element.8.refs_2_), custom_call_target="tpu_custom_call" | custom-call | tf_op jit(solution)/shard_map/results/pallas_call | solution.py:391

commit v7 on v6

--- a/solution.py
+++ b/solution.py
@@ -72,10 +72,10 @@
         )
 
     def ring_sem(w, j):
-        return ring_r.at[j // 2 - 1 if w == DY else 3 + j // 6]
-
-    def pair_sem(j):
-        return pair_r.at[(j // 2 + 1) // 2]
+        return ring_r.at[j // 2 - 1 if w == DY else 3 - 3 * (j // 6)]
+
+    def pair_sem(w, j):
+        return pair_r.at[j // 2 % 2 if w == DY else 1 - j // 6]
 
     def ring_own(w, j):
         h = {2: 0, 3: 1, 4: 1, 5: 0}[j]
@@ -90,7 +90,7 @@
 
     def to_partner(w, j):
         src = own_half(w, j) if j < 2 else of_core(gathered[w], j, core)
-        return remote(src, of_core(gathered[w], j, core), sent.at[0], pair_sem(j), partner)
+        return remote(src, of_core(gathered[w], j, core), sent.at[0], pair_sem(w, j), partner)
 
     def service(w, j):
         count = 4 if w == X and j == 2 else 2
@@ -109,12 +109,12 @@
     def start_rows(w, j):
         def arrived(pairs):
             some = gathered[w].at[pl.ds(0, pairs // 2)]
-            remote(some, some, sent.at[0], pair_sem(j), partner).wait_recv()
+            remote(some, some, sent.at[0], pair_sem(w, j), partner).wait_recv()
 
         if w == DY:
             pl.when(j % 2 == 0)(lambda: arrived(2))
         else:
-            for first, pairs in ((0, 2), (2, 4), (6, 2)):
+            for first, pairs in ((0, 6), (6, 2)):
                 pl.when(j == first)(functools.partial(arrived, pairs))
 
         slot = j % 2
@@ -193,8 +193,6 @@
             service(DY, 2)
             ring_own(X, 2).start()
             ring_own(X, 3).start()
-            to_partner(X, 0).start()
-            to_partner(X, 1).start()
 
         @pl.when(i == 3)
         def _():
@@ -267,6 +265,8 @@
 
             ring_sum(i).start()
 
+    to_partner(X, 0).start()
+    to_partner(X, 1).start()
     service(X, 2)
     start_rows(X, 0)
     pair_sum(PAIRS - 1).wait_send()
@@ -382,7 +382,7 @@
                 pltpu.VMEM((2, half, d), BF16),
                 pltpu.VMEM((4, half, d), BF16),
                 pltpu.VMEM((2, half, d), BF16),
-                dma((2,)), dma((5,)), dma((3,)), dma((1,)), dma((2,)), dma((1,)), dma((2,)), dma((2,)),
+                dma((2,)), dma((4,)), dma((2,)), dma((1,)), dma((2,)), dma((1,)), dma((2,)), dma((2,)),
             ],
             compiler_params=pltpu.CompilerParams(collective_id=0, has_side_effects=True, vmem_limit_bytes=VMEM_LIMIT),
             name="mlp_backward",

time: 212 us -> 212 us (level)
  no operation moved by 1% of the time
where the time goes in v7:
time: 212 us
  Pallas kernels  212 us (100%)
    pallas_call x1, Pallas kernels, step(): pl.pallas_call(functools.partial(kernel, n), out_shape=[pltpu.VMEM(s, BF1...  208 us

profile of v7, /device:TPU:112, one launch (start us, length us, event | category | flops | bytes accessed | tf_op | source)
XLA Modules:
  0.0 212.1 jit_solution(472738368852368440)
XLA Ops:
  0.6 207.7 %mlp_backward.1 = (bf16[512,2048]{1,0:T(8,128)(2,1)S(1)}, bf16[2048,1024]{1,0:T(8,128)(2,1)S(1)}, bf16[1024,2048]{1,0:T(8,128)(2,1)S(1)}, bf16[8,512,2048]{2,1,0:T(8,128)(2,1)}, bf16[8,512,2048]{2,1,0:T(8,128)(2,1)}) custom-call(bf16[512,2048]{1,0:T(8,128)(2,1)} %x.1, bf16[512,2048]{1,0:T(8,128)(2,1)} %dy.1, bf16[4096,1024]{1,0:T(8,128)(2,1)} %pre.1, ...), custom_call_target="tpu_custom_call" | custom-call | tf_op jit(solution)/shard_map/mlp_backward/pallas_call | solution.py:364
  208.4 3.8 %results.1 = (bf16[512,2048]{1,0:T(8,128)(2,1)}, bf16[2048,1024]{1,0:T(8,128)(2,1)}, bf16[1024,2048]{1,0:T(8,128)(2,1)}) custom-call(bf16[512,2048]{1,0:T(8,128)(2,1)S(1)} %get-tuple-element.6.refs_0_, bf16[2048,1024]{1,0:T(8,128)(2,1)S(1)} %get-tuple-element.7.refs_1_, bf16[1024,2048]{1,0:T(8,128)(2,1)S(1)} %get-tuple-element.8.refs_2_), custom_call_target="tpu_custom_call" | custom-call | tf_op jit(solution)/shard_map/results/pallas_call | solution.py:391

commit v8 on v7

--- a/solution.py
+++ b/solution.py
@@ -157,7 +157,7 @@
         return remote(st_ring.at[ref], chain_buf.at[ref], sent.at[0], ch_r.at[q], left if b == 0 else right)
 
     barrier = pltpu.get_barrier_semaphore()
-    for dev in (left, right, partner):
+    for dev in (partner, left, right):
         pl.semaphore_signal(barrier, inc=1, device_id={"tp": dev}, device_id_type=MESH)
     pl.semaphore_wait(barrier, 3)
 

time: 212 us -> 212 us (level)
  no operation moved by 1% of the time
where the time goes in v8:
time: 212 us
  Pallas kernels  211 us (100%)
    pallas_call x1, Pallas kernels, step(): pl.pallas_call(functools.partial(kernel, n), out_shape=[pltpu.VMEM(s, BF1...  208 us

profile of v8, /device:TPU:112, one launch (start us, length us, event | category | flops | bytes accessed | tf_op | source)
XLA Modules:
  0.0 212.1 jit_solution(11851434769028872343)
XLA Ops:
  0.6 207.7 %mlp_backward.1 = (bf16[512,2048]{1,0:T(8,128)(2,1)S(1)}, bf16[2048,1024]{1,0:T(8,128)(2,1)S(1)}, bf16[1024,2048]{1,0:T(8,128)(2,1)S(1)}, bf16[8,512,2048]{2,1,0:T(8,128)(2,1)}, bf16[8,512,2048]{2,1,0:T(8,128)(2,1)}) custom-call(bf16[512,2048]{1,0:T(8,128)(2,1)} %x.1, bf16[512,2048]{1,0:T(8,128)(2,1)} %dy.1, bf16[4096,1024]{1,0:T(8,128)(2,1)} %pre.1, ...), custom_call_target="tpu_custom_call" | custom-call | tf_op jit(solution)/shard_map/mlp_backward/pallas_call | solution.py:364
  208.3 3.8 %results.1 = (bf16[512,2048]{1,0:T(8,128)(2,1)}, bf16[2048,1024]{1,0:T(8,128)(2,1)}, bf16[1024,2048]{1,0:T(8,128)(2,1)}) custom-call(bf16[512,2048]{1,0:T(8,128)(2,1)S(1)} %get-tuple-element.6.refs_0_, bf16[2048,1024]{1,0:T(8,128)(2,1)S(1)} %get-tuple-element.7.refs_1_, bf16[1024,2048]{1,0:T(8,128)(2,1)S(1)} %get-tuple-element.8.refs_2_), custom_call_target="tpu_custom_call" | custom-call | tf_op jit(solution)/shard_map/results/pallas_call | solution.py:391
